TPU v7x, 256 devices: a whole 4x4x8 slice. The times are simulated.
256 devices in a mesh: lat: 8 (over x_lo, y), lon: 32 (over z, x_hi, core).
Axes of the slice: x: 4 (x_hi: 2, x_lo: 2; x = x_hi * 2 + x_lo), y: 4, z: 8, core: 2. Of those that a mesh axis runs over, the one named last changes fastest.
Arguments:
- field: bfloat16 [256, 1024, 512], P('lat', 'lon'), may hold values from -6 to 6
- qkv_fine: bfloat16 [512, 1536], replicated, may hold values from -0.35355339 to 0.35355339
- proj_fine: bfloat16 [512, 512], replicated, may hold values from -0.25 to 0.25
- up_fine: bfloat16 [512, 2048], replicated, may hold values from -0.25 to 0.25
- down_fine: bfloat16 [2048, 512], replicated, may hold values from -0.125 to 0.125
- merge_weight: bfloat16 [2048, 1024], replicated, may hold values from -0.15467961 to 0.15467961
- qkv_coarse: bfloat16 [1024, 3072], P(None, 'lon'), may hold values from -0.25 to 0.25
- proj_coarse: bfloat16 [1024, 1024], P(None, 'lon'), may hold values from -0.1875 to 0.1875
Outputs:
- fine_out: bfloat16 [256, 1024, 512], P('lat', 'lon')
- coarse_out: bfloat16 [128, 512, 1024], P('lat', 'lon')
All inputs are finite; a program needn't handle non-finite values.
Results may differ from a plain program's by a relative error of at most 0.018.
Values may be sent and summed in bfloat16 or wider, within the bound.
A program may use at most 128 MiB of HBM per device.

v0:
```python
import jax
import jax.numpy as jnp
from jax import lax
from jax.experimental import pallas as pl
from jax.experimental.pallas import tpu as pltpu
from jax.sharding import PartitionSpec as P

MESH = pl.DeviceIdType.MESH
BF = jnp.bfloat16
F32 = jnp.float32
OFFSETS = (0, -1, 1, -2, 2, -3, 3, 4)
CHUNKS = ((0, 1), (1, 2), (3, 2), (5, 2), (7, 1))


def norm(v):
    center = v - jnp.mean(v, axis=-1, keepdims=True)
    spread = jnp.mean(center * center, axis=-1, keepdims=True)
    return center * lax.rsqrt(spread + 1e-05)


def dot(a, b):
    return jnp.dot(a, b, preferred_element_type=F32)


def attend_pair(keys, qt, vt, bias):
    zero = jnp.zeros((64, 256), BF)
    outs = []
    for half in range(2):
        part = qt[64 * half : 64 * half + 64]
        padded = jnp.concatenate([part, zero] if half == 0 else [zero, part], axis=0)
        scores = dot(keys, padded) + bias
        top = jnp.max(scores, axis=0, keepdims=True)
        p = jnp.exp(scores - top)
        total = jnp.sum(p, axis=0, keepdims=True)
        o = dot(vt[64 * half : 64 * half + 64], p.astype(BF))
        outs.append(o * (1.0 / total))
    return jnp.concatenate(outs, axis=0)


def kernel(
    field, wqkv_h, wproj_h, wup_h, wdown_h, wmerge_h, wsh,
    fine_out, coarse_out,
    wqkv, wproj, wup, wdown, wmerge,
    fv, xr, mr, mo, fo, fs, jn, mg, cr, cxt, wall, qkvt, ot, cm, cmo, co, pt,
    lsem, osem, hs, hr, bs, br, cs, cq, ds_, dr, zs, zr, xs, xq, ps, pr, es, er, gs, gr,
):
    lat = lax.axis_index("lat")
    lon = lax.axis_index("lon")
    xlo = lat // 4
    y = lat % 4
    z = lon // 4
    xh = (lon // 2) % 2
    c = lon % 2
    west = (lat, (lon + 31) % 32)
    east = (lat, (lon + 1) % 32)
    north = ((lat + 7) % 8, lon)
    south = ((lat + 1) % 8, lon)
    northwest = ((lat + 7) % 8, (lon + 31) % 32)
    southeast = ((lat + 1) % 8, (lon + 1) % 32)
    zup = (lat, ((z + 1) % 8) * 4 + xh * 2 + c)
    zdn = (lat, ((z + 7) % 8) * 4 + xh * 2 + c)
    cross = ((1 - xlo) * 4 + y, z * 4 + (1 - xh) * 2 + c)
    pair = ((1 - xlo) * 4 + y, lon)
    twin = (lat, z * 4 + xh * 2 + (1 - c))

    def local(src, dst, at):
        copy = pltpu.make_async_copy(src, dst, lsem.at[at])
        copy.start()
        return copy

    sent = []

    def remote(src, dst, ssem, rsem, at, device):
        copy = pltpu.make_async_remote_copy(
            src_ref=src, dst_ref=dst, send_sem=ssem.at[at], recv_sem=rsem.at[at],
            device_id=device, device_id_type=MESH,
        )
        copy.start()
        sent.append(copy)
        return copy

    own_x = local(field.at[pl.ds(8, 24), pl.ds(1, 3)], xr.at[pl.ds(0, 24), pl.ds(0, 3)], 0)
    l_qkv = local(wqkv_h, wqkv, 1)
    own_w = local(wsh, wall.at[xh, c, 0], 7)
    own_f = local(field, fv, 2)
    l_proj = local(wproj_h, wproj, 3)
    l_up = local(wup_h, wup, 4)
    l_down = local(wdown_h, wdown, 5)
    l_merge = local(wmerge_h, wmerge, 6)

    barrier = pltpu.get_barrier_semaphore()
    peers = (west, east, north, south, northwest, southeast, zup, zdn, cross, pair, twin)
    for peer in peers:
        pl.semaphore_signal(barrier, inc=1, device_id=peer, device_id_type=MESH)
    pl.semaphore_wait(barrier, len(peers))

    h = [
        remote(field.at[pl.ds(8, 24), 0], xr.at[pl.ds(0, 24), 3], hs, hr, 0, west),
        remote(field.at[pl.ds(0, 8), pl.ds(1, 3)], xr.at[pl.ds(24, 8), pl.ds(0, 3)], hs, hr, 1, north),
        remote(field.at[pl.ds(0, 8), 0], xr.at[pl.ds(24, 8), 3], hs, hr, 2, northwest),
    ]

    zc, xc, pc, ec, gc = {}, {}, {}, {}, {}

    def send_z(step):
        if step == 0:
            zc[0] = remote(wsh, wall.at[xh, c, 1], zs, zr, 0, zup)
            zc[1] = remote(wsh, wall.at[xh, c, 2], zs, zr, 1, zdn)
        elif step < 3:
            a = 2 * step
            zc[a] = remote(wall.at[xh, c, a - 1], wall.at[xh, c, a + 1], zs, zr, a, zup)
            zc[a + 1] = remote(wall.at[xh, c, a], wall.at[xh, c, a + 2], zs, zr, a + 1, zdn)
        else:
            zc[6] = remote(wall.at[xh, c, 5, 0], wall.at[xh, c, 7, 0], zs, zr, 6, zup)
            zc[7] = remote(wall.at[xh, c, 6, 1], wall.at[xh, c, 7, 1], zs, zr, 7, zdn)

    def own_chunk(k):
        at, n = CHUNKS[k]
        if k == 0:
            src_half, src = wsh.at[xlo], wsh
            dst_half, dst = wall.at[xh, c, 0, xlo], wall.at[xh, c, 0]
        else:
            src_half = dst_half = wall.at[xh, c, pl.ds(at, n), xlo]
            src = dst = wall.at[xh, c, pl.ds(at, n)]
        xc[k] = remote(src_half, dst_half, xs, xq, k, cross)
        ec[k] = remote(src, dst, es, er, k, twin)

    def pass_cross(k):
        at, n = CHUNKS[k]
        xc[k].wait_recv()
        ref = wall.at[1 - xh, c, pl.ds(at, n), 1 - xlo]
        pc[k] = remote(ref, ref, ps, pr, k, pair)

    def pass_twin(k):
        at, n = CHUNKS[k]
        pc[k].wait_recv()
        ref = wall.at[1 - xh, c, pl.ds(at, n)]
        gc[k] = remote(ref, ref, gs, gr, k, twin)

    send_z(0)
    own_chunk(0)

    def forward(k):
        zc[2 * k - 2].wait_recv()
        zc[2 * k - 1].wait_recv()
        if k < 4:
            send_z(k)
        own_chunk(k)
        pass_cross(k - 1)
        if k >= 2:
            pass_twin(k - 2)

    off_half = (lax.broadcasted_iota(jnp.int32, (256, 256), 0) >= 128) != (
        lax.broadcasted_iota(jnp.int32, (256, 256), 1) >= 128
    )
    edge = lat == 7

    def fine_window(wr, wc):
        lift = jnp.where(jnp.logical_and(edge, wr == 1), F32(-1e30), F32(0.0))
        bias = jnp.where(off_half, lift, F32(0.0))
        x = xr[pl.ds(16 * wr, 16), pl.ds(2 * wc, 2)].astype(F32).reshape(256, 512)
        xn = norm(x).astype(BF)
        q = (dot(xn, wqkv[:, 0:512])).astype(BF).astype(F32) * 0.125
        keys = dot(xn, wqkv[:, 512:1024]).astype(BF)
        v = dot(xn, wqkv[:, 1024:1536])
        qt = q.T.astype(BF)
        vt = v.T.astype(BF)
        outs = []
        for j in range(4):
            cut = slice(128 * j, 128 * j + 128)
            outs.append(attend_pair(keys[:, cut], qt[cut], vt[cut], bias).T)
        res = jnp.concatenate(outs, axis=1)
        mr[pl.ds(16 * wr, 16), pl.ds(2 * wc, 2)] = res.reshape(16, 2, 8, 512).astype(BF)

    own_x.wait()
    l_qkv.wait()
    own_w.wait()
    fine_window(0, 0)
    for copy in h:
        copy.wait_recv()

    b = [None] * 5

    @pl.loop(0, 3)
    def _(step):
        wr = jnp.where(step == 1, 0, 1)
        wc = jnp.where(step == 2, 0, 1)
        fine_window(wr, wc)

    forward(1)
    b[0] = remote(mr.at[pl.ds(0, 24), 3], mo.at[pl.ds(8, 24), 0], bs, br, 0, east)
    b[1] = remote(mr.at[pl.ds(24, 8), pl.ds(0, 3)], mo.at[pl.ds(0, 8), pl.ds(1, 3)], bs, br, 1, south)
    b[2] = remote(mr.at[pl.ds(24, 8), 3], mo.at[pl.ds(0, 8), 0], bs, br, 2, southeast)
    mo[pl.ds(8, 24), pl.ds(1, 3)] = mr[pl.ds(0, 24), pl.ds(0, 3)]
    for copy in (own_f, l_proj, l_up, l_down, l_merge):
        copy.wait()
    for copy in b[:3]:
        copy.wait_recv()

    def fine_chunk(k):
        rows = pl.ds(8 * k, 8)
        x = fv[rows].astype(F32).reshape(256, 512)
        mx = mo[rows].astype(F32).reshape(256, 512).astype(BF)
        att = (x + dot(mx, wproj[...])).astype(BF).astype(F32)
        n = norm(att).astype(BF)
        acc = att
        for s in range(4):
            cut = slice(512 * s, 512 * s + 512)
            hid = jax.nn.gelu(dot(n, wup[:, cut])).astype(BF)
            acc = acc + dot(hid, wdown[cut, :])
        out = acc.astype(BF)
        out32 = out.astype(F32)
        fo[rows] = out32.reshape(8, 4, 8, 512).astype(BF)
        for t in range(4):
            fs[t] = out32[:, 128 * t : 128 * t + 128]
        for i in range(4):
            joined = jnp.concatenate(
                [
                    fs[t, pl.ds(64 * i + 32 * (p % 2) + p // 2, 16, stride=2), :]
                    for p in range(4)
                    for t in range(4)
                ],
                axis=1,
            )
            jn[pl.ds(pl.multiple_of(64 * k + 16 * i, 16), 16), :] = norm(joined).astype(BF)

    @pl.loop(0, 2)
    def _(k):
        fine_chunk(k)

    forward(2)

    @pl.loop(2, 4)
    def _(k):
        fine_chunk(k)

    forward(3)
    out_f = pltpu.make_async_copy(fo, fine_out, osem.at[0])
    out_f.start()

    @pl.loop(0, 4)
    def _(s):
        cut = pl.ds(pl.multiple_of(256 * s, 256), 256)
        m = dot(jn[...], wmerge[:, cut])
        mg[:, :, :, cut] = m.reshape(16, 2, 8, 256).astype(BF)

    a = [
        remote(mg.at[pl.ds(8, 8), 0], cr.at[pl.ds(0, 8), 1], cs, cq, 0, west),
        remote(mg.at[pl.ds(0, 8), 1], cr.at[pl.ds(8, 8), 0], cs, cq, 1, north),
        remote(mg.at[pl.ds(0, 8), 0], cr.at[pl.ds(8, 8), 1], cs, cq, 2, northwest),
    ]
    cr[pl.ds(0, 8), 0] = mg[pl.ds(8, 8), 1]
    forward(4)
    for copy in a:
        copy.wait_recv()
    cxt[...] = norm(cr[...].astype(F32).reshape(256, 1024)).T.astype(BF)
    pass_cross(4)
    pass_twin(3)
    pass_twin(4)
    for k in range(5):
        ec[k].wait_recv()
    for k in range(5):
        gc[k].wait_recv()

    @pl.loop(0, 4)
    def _(g):
        for r2 in range(2):
            w = wall[g // 2, g % 2, pl.ds(4 * r2, 4)].reshape(512, 1024)
            got = dot(w, cxt[...]).astype(BF)
            for i in range(4):
                slot = ((z + OFFSETS[4 * r2 + i] + 8) % 8) * 4 + g
                at = pl.multiple_of(96 * slot, 32)
                qkvt[pl.ds(at, 96), :] = got[128 * i : 128 * i + 96]
                pt[pl.ds(pl.multiple_of(32 * slot, 32), 32), :] = wall[
                    g // 2, g % 2, 4 * r2 + i, 1, pl.ds(32, 32), :
                ]

    c_lift = jnp.where(edge, F32(-1e30), F32(0.0))

    @pl.loop(0, 8)
    def _(j):
        bias = jnp.where(off_half, c_lift, F32(0.0))
        at = pl.multiple_of(128 * j, 128)
        qt = (qkvt[pl.ds(at, 128), :].astype(F32) * 0.125).astype(BF)
        keys = qkvt[pl.ds(at + 1024, 128), :].astype(F32).T.astype(BF)
        vt = qkvt[pl.ds(at + 2048, 128), :]
        o = attend_pair(keys, qt, vt, bias).T
        cm[:, :, :, pl.ds(at, 128)] = o.reshape(16, 2, 8, 128).astype(BF)

    d = [
        remote(cm.at[pl.ds(0, 8), 1], cmo.at[pl.ds(8, 8), 0], ds_, dr, 0, east),
        remote(cm.at[pl.ds(8, 8), 0], cmo.at[pl.ds(0, 8), 1], ds_, dr, 1, south),
        remote(cm.at[pl.ds(8, 8), 1], cmo.at[pl.ds(0, 8), 0], ds_, dr, 2, southeast),
    ]
    cmo[pl.ds(8, 8), 1] = cm[pl.ds(0, 8), 0]
    for copy in d:
        copy.wait_recv()
    mixed = cmo[...].astype(F32).reshape(256, 1024).astype(BF)
    ot[...] = mixed

    @pl.loop(0, 4)
    def _(s):
        at = pl.multiple_of(256 * s, 256)
        got = lax.dot_general(
            ot[...], pt[pl.ds(at, 256), :], (((1,), (1,)), ((), ())), preferred_element_type=F32
        )
        cut = pl.ds(at, 256)
        res = mg[:, :, :, cut].astype(F32) + got.reshape(16, 2, 8, 256)
        co[:, :, :, cut] = res.astype(BF)

    out_c = pltpu.make_async_copy(co, coarse_out, osem.at[1])
    out_c.start()
    for copy in sent:
        copy.wait_send()
    out_f.wait()
    out_c.wait()


def body(field, qkv_fine, proj_fine, up_fine, down_fine, merge_weight, qkv_coarse, proj_coarse):
    shard = jnp.concatenate([qkv_coarse.T, proj_coarse.T], axis=0).reshape(2, 64, 1024)
    any_spec = pl.BlockSpec(memory_space=pl.ANY)
    dma = pltpu.SemaphoreType.DMA
    vm = pltpu.VMEM
    fine, coarse = pl.pallas_call(
        kernel,
        out_shape=(
            jax.ShapeDtypeStruct((32, 4, 8, 512), BF),
            jax.ShapeDtypeStruct((16, 2, 8, 1024), BF),
        ),
        in_specs=[any_spec] * 7,
        out_specs=(any_spec, any_spec),
        scratch_shapes=[
            vm((512, 1536), BF), vm((512, 512), BF), vm((512, 2048), BF), vm((2048, 512), BF),
            vm((2048, 1024), BF),
            vm((32, 4, 8, 512), BF), vm((32, 4, 8, 512), BF), vm((32, 4, 8, 512), BF),
            vm((32, 4, 8, 512), BF), vm((32, 4, 8, 512), BF),
            vm((4, 256, 128), F32), vm((256, 2048), BF),
            vm((16, 2, 8, 1024), BF), vm((16, 2, 8, 1024), BF), vm((1024, 256), BF),
            vm((2, 2, 8, 2, 64, 1024), BF), vm((3072, 256), BF), vm((256, 1024), BF),
            vm((16, 2, 8, 1024), BF), vm((16, 2, 8, 1024), BF), vm((16, 2, 8, 1024), BF),
            vm((1024, 1024), BF),
            dma((8,)), dma((2,)),
            dma((3,)), dma((3,)), dma((3,)), dma((3,)), dma((3,)), dma((3,)), dma((3,)), dma((3,)),
            dma((8,)), dma((8,)), dma((5,)), dma((5,)), dma((5,)), dma((5,)),
            dma((5,)), dma((5,)), dma((5,)), dma((5,)),
        ],
        compiler_params=pltpu.CompilerParams(
            collective_id=0, has_side_effects=True, vmem_limit_bytes=60 * 1024 * 1024
        ),
        name="encoder",
    )(field.reshape(32, 4, 8, 512), qkv_fine, proj_fine, up_fine, down_fine, merge_weight, shard)
    return fine.reshape(32, 32, 512), coarse.reshape(16, 16, 1024)


def solution(mesh):
    in_specs = (P("lat", "lon", None), P(), P(), P(), P(), P(), P(None, "lon"), P(None, "lon"))
    out_specs = (P("lat", "lon", None), P("lat", "lon", None))
    return jax.shard_map(body, mesh=mesh, in_specs=in_specs, out_specs=out_specs, check_vma=False)
```

profile of v0, /device:TPU:8, one launch (start us, length us, event | category | flops | bytes accessed | tf_op | source)
XLA Modules:
  0.0 99.9 jit_solution(15286727171824971699)
XLA Ops:
  0.6 1.7 %pad_maximum_fusion = bf16[128,1024]{1,0:T(8,128)(2,1)} fusion(bf16[32,1024]{1,0:T(8,128)(2,1)} %bitcast.11, bf16[96,1024]{1,0:T(8,128)(2,1)} %bitcast.10), kind=kLoop, calls=%fused_computation | loop fusion | flops 524288 | bytes 524288 | tf_op jit(solution)/shard_map/concatenate | solution.py:320
  2.3 94.4 %encoder.1 = (bf16[32,4,8,512]{3,2,1,0:T(8,128)(2,1)}, bf16[16,2,8,1024]{3,2,1,0:T(8,128)(2,1)}) custom-call(bf16[32,4,8,512]{3,2,1,0:T(8,128)(2,1)} %bitcast.6, bf16[512,1536]{1,0:T(8,128)(2,1)} %wqkv_h.1, bf16[512,512]{1,0:T(8,128)(2,1)} %wproj_h.1, bf16[512,2048]{1,0:T(8,128)(2,1)} %wup_h.1, bf16[2048,512]{1,0:T(8,128)(2,1)} %wdown_h.1, ...), custom_call_target="tpu_custom_call" | custom-call | tf_op jit(solution)/shard_map/encoder/pallas_call | solution.py:324
  96.7 0.0 copy-start
  96.8 2.4 %copy.12 = bf16[32,32,512]{2,1,0:T(8,128)(2,1)} copy(bf16[32,32,512]{2,1,0:T(8,128)(2,1)} %bitcast.8) | data formatting | bytes 2097152
  99.1 0.0 copy-done
  99.1 0.8 copy.13
Async XLA Ops:
  96.7 2.4 %copy-start = (bf16[16,2,8,1024]{3,2,1,0:T(8,128)(2,1)S(1)}, bf16[16,2,8,1024]{3,2,1,0:T(8,128)(2,1)}, u32[]{:S(2)}) copy-start(bf16[16,2,8,1024]{3,2,1,0:T(8,128)(2,1)} %get-tuple-element.5) | copy-start | bytes 1572868
where the time goes:
time: 100 us; the launch traced here: 99.9 us
  Pallas kernels  94.4 us (94%)
  local copies, waits for them, and re-layouts  3.16 us (3%)
  other arithmetic  1.69 us (2%)
    pallas_call x1, Pallas kernels, body(): pl.pallas_call(kernel, out_shape=(jax.ShapeDtypeStruct((32, 4, 8, 512), B...  94.4 us
    unnamed x4, local copies, waits for them, and re-layouts  3.16 us

commit v1 on v0

--- a/solution.py
+++ b/solution.py
@@ -38,9 +38,9 @@
 
 
 def kernel(
-    field, wqkv_h, wproj_h, wup_h, wdown_h, wmerge_h, wsh,
+    field, wqkv_h, wproj_h, wup_h, wdown_h, wmerge_h, cqkv_h, cproj_h,
     fine_out, coarse_out,
-    wqkv, wproj, wup, wdown, wmerge,
+    wqkv, wproj, wup, wdown, wmerge, cqkv, cproj,
     fv, xr, mr, mo, fo, fs, jn, mg, cr, cxt, wall, qkvt, ot, cm, cmo, co, pt,
     lsem, osem, hs, hr, bs, br, cs, cq, ds_, dr, zs, zr, xs, xq, ps, pr, es, er, gs, gr,
 ):
@@ -80,8 +80,9 @@
         return copy
 
     own_x = local(field.at[pl.ds(8, 24), pl.ds(1, 3)], xr.at[pl.ds(0, 24), pl.ds(0, 3)], 0)
+    own_q = local(cqkv_h, cqkv, 7)
+    own_p = local(cproj_h, cproj, 8)
     l_qkv = local(wqkv_h, wqkv, 1)
-    own_w = local(wsh, wall.at[xh, c, 0], 7)
     own_f = local(field, fv, 2)
     l_proj = local(wproj_h, wproj, 3)
     l_up = local(wup_h, wup, 4)
@@ -104,8 +105,8 @@
 
     def send_z(step):
         if step == 0:
-            zc[0] = remote(wsh, wall.at[xh, c, 1], zs, zr, 0, zup)
-            zc[1] = remote(wsh, wall.at[xh, c, 2], zs, zr, 1, zdn)
+            zc[0] = remote(wall.at[xh, c, 0], wall.at[xh, c, 1], zs, zr, 0, zup)
+            zc[1] = remote(wall.at[xh, c, 0], wall.at[xh, c, 2], zs, zr, 1, zdn)
         elif step < 3:
             a = 2 * step
             zc[a] = remote(wall.at[xh, c, a - 1], wall.at[xh, c, a + 1], zs, zr, a, zup)
@@ -116,14 +117,10 @@
 
     def own_chunk(k):
         at, n = CHUNKS[k]
-        if k == 0:
-            src_half, src = wsh.at[xlo], wsh
-            dst_half, dst = wall.at[xh, c, 0, xlo], wall.at[xh, c, 0]
-        else:
-            src_half = dst_half = wall.at[xh, c, pl.ds(at, n), xlo]
-            src = dst = wall.at[xh, c, pl.ds(at, n)]
-        xc[k] = remote(src_half, dst_half, xs, xq, k, cross)
-        ec[k] = remote(src, dst, es, er, k, twin)
+        half = wall.at[xh, c, pl.ds(at, n), xlo]
+        full = wall.at[xh, c, pl.ds(at, n)]
+        xc[k] = remote(half, half, xs, xq, k, cross)
+        ec[k] = remote(full, full, es, er, k, twin)
 
     def pass_cross(k):
         at, n = CHUNKS[k]
@@ -137,6 +134,12 @@
         ref = wall.at[1 - xh, c, pl.ds(at, n)]
         gc[k] = remote(ref, ref, gs, gr, k, twin)
 
+    own_q.wait()
+    own_p.wait()
+    for t in range(4):
+        rows = slice(256 * t, 256 * t + 256)
+        shard = jnp.concatenate([cqkv[rows, :].astype(F32), cproj[rows, :].astype(F32)], axis=1)
+        wall[xh, c, 0, :, :, rows] = shard.T.astype(BF).reshape(2, 64, 256)
     send_z(0)
     own_chunk(0)
 
@@ -174,33 +177,28 @@
 
     own_x.wait()
     l_qkv.wait()
-    own_w.wait()
     fine_window(0, 0)
-    for copy in h:
-        copy.wait_recv()
-
-    b = [None] * 5
-
-    @pl.loop(0, 3)
-    def _(step):
-        wr = jnp.where(step == 1, 0, 1)
-        wc = jnp.where(step == 2, 0, 1)
-        fine_window(wr, wc)
-
+    h[0].wait_recv()
+    fine_window(0, 1)
+    b = [remote(mr.at[pl.ds(0, 16), 3], mo.at[pl.ds(8, 16), 0], bs, br, 0, east)]
+    h[1].wait_recv()
+    h[2].wait_recv()
     forward(1)
-    b[0] = remote(mr.at[pl.ds(0, 24), 3], mo.at[pl.ds(8, 24), 0], bs, br, 0, east)
-    b[1] = remote(mr.at[pl.ds(24, 8), pl.ds(0, 3)], mo.at[pl.ds(0, 8), pl.ds(1, 3)], bs, br, 1, south)
-    b[2] = remote(mr.at[pl.ds(24, 8), 3], mo.at[pl.ds(0, 8), 0], bs, br, 2, southeast)
+    fine_window(1, 0)
+    b.append(remote(mr.at[pl.ds(24, 8), pl.ds(0, 2)], mo.at[pl.ds(0, 8), pl.ds(1, 2)], bs, br, 1, south))
+    fine_window(1, 1)
+    b.append(remote(mr.at[pl.ds(16, 8), 3], mo.at[pl.ds(24, 8), 0], bs, br, 2, east))
+    b.append(remote(mr.at[pl.ds(24, 8), 2], mo.at[pl.ds(0, 8), 3], bs, br, 3, south))
+    b.append(remote(mr.at[pl.ds(24, 8), 3], mo.at[pl.ds(0, 8), 0], bs, br, 4, southeast))
+    forward(2)
     mo[pl.ds(8, 24), pl.ds(1, 3)] = mr[pl.ds(0, 24), pl.ds(0, 3)]
     for copy in (own_f, l_proj, l_up, l_down, l_merge):
         copy.wait()
-    for copy in b[:3]:
-        copy.wait_recv()
-
-    def fine_chunk(k):
-        rows = pl.ds(8 * k, 8)
-        x = fv[rows].astype(F32).reshape(256, 512)
-        mx = mo[rows].astype(F32).reshape(256, 512).astype(BF)
+
+    def fine_quarter(qr, qc):
+        rows, cols = pl.ds(16 * qr, 16), pl.ds(2 * qc, 2)
+        x = fv[rows, cols].astype(F32).reshape(256, 512)
+        mx = mo[rows, cols].astype(F32).reshape(256, 512).astype(BF)
         att = (x + dot(mx, wproj[...])).astype(BF).astype(F32)
         n = norm(att).astype(BF)
         acc = att
@@ -208,95 +206,109 @@
             cut = slice(512 * s, 512 * s + 512)
             hid = jax.nn.gelu(dot(n, wup[:, cut])).astype(BF)
             acc = acc + dot(hid, wdown[cut, :])
-        out = acc.astype(BF)
-        out32 = out.astype(F32)
-        fo[rows] = out32.reshape(8, 4, 8, 512).astype(BF)
+        out32 = acc.astype(BF).astype(F32)
+        fo[rows, cols] = out32.reshape(16, 2, 8, 512).astype(BF)
         for t in range(4):
             fs[t] = out32[:, 128 * t : 128 * t + 128]
         for i in range(4):
             joined = jnp.concatenate(
                 [
-                    fs[t, pl.ds(64 * i + 32 * (p % 2) + p // 2, 16, stride=2), :]
-                    for p in range(4)
-                    for t in range(4)
+                    jnp.concatenate(
+                        [
+                            fs[t, pl.ds(64 * i + 32 * r + 16 * (p % 2) + p // 2, 8, stride=2), :]
+                            for p in range(4)
+                            for t in range(4)
+                        ],
+                        axis=1,
+                    )
+                    for r in range(2)
                 ],
-                axis=1,
+                axis=0,
             )
-            jn[pl.ds(pl.multiple_of(64 * k + 16 * i, 16), 16), :] = norm(joined).astype(BF)
-
-    @pl.loop(0, 2)
-    def _(k):
-        fine_chunk(k)
-
-    forward(2)
-
-    @pl.loop(2, 4)
-    def _(k):
-        fine_chunk(k)
-
+            at = pl.multiple_of(64 * (2 * qr + qc) + 16 * i, 16)
+            jn[pl.ds(at, 16), :] = norm(joined).astype(BF)
+
+    def merge(first, count):
+        @pl.loop(0, 4)
+        def _(s):
+            cut = pl.ds(pl.multiple_of(256 * s, 256), 256)
+            m = dot(jn[64 * first : 64 * (first + count), :], wmerge[:, cut])
+            mg[first : first + count, :, :, cut] = m.reshape(count, 8, 8, 256).astype(BF)
+
+    fine_quarter(1, 1)
+    b[0].wait_recv()
+    b[2].wait_recv()
+    fine_quarter(1, 0)
+    for at in (1, 3, 4):
+        b[at].wait_recv()
+    fine_quarter(0, 1)
     forward(3)
+    fine_quarter(0, 0)
+    merge(0, 3)
+    a = [
+        remote(mg.at[2], cr.at[1], cs, cq, 0, west),
+        remote(mg.at[1], cr.at[2], cs, cq, 1, north),
+        remote(mg.at[0], cr.at[3], cs, cq, 2, northwest),
+    ]
     out_f = pltpu.make_async_copy(fo, fine_out, osem.at[0])
     out_f.start()
-
-    @pl.loop(0, 4)
-    def _(s):
-        cut = pl.ds(pl.multiple_of(256 * s, 256), 256)
-        m = dot(jn[...], wmerge[:, cut])
-        mg[:, :, :, cut] = m.reshape(16, 2, 8, 256).astype(BF)
-
-    a = [
-        remote(mg.at[pl.ds(8, 8), 0], cr.at[pl.ds(0, 8), 1], cs, cq, 0, west),
-        remote(mg.at[pl.ds(0, 8), 1], cr.at[pl.ds(8, 8), 0], cs, cq, 1, north),
-        remote(mg.at[pl.ds(0, 8), 0], cr.at[pl.ds(8, 8), 1], cs, cq, 2, northwest),
-    ]
-    cr[pl.ds(0, 8), 0] = mg[pl.ds(8, 8), 1]
     forward(4)
+    merge(3, 1)
+    cr[0] = mg[3]
+    pass_cross(4)
     for copy in a:
         copy.wait_recv()
     cxt[...] = norm(cr[...].astype(F32).reshape(256, 1024)).T.astype(BF)
-    pass_cross(4)
+
+    def project(gx, gc_):
+        for r2 in range(2):
+            w = wall[gx, gc_, pl.ds(4 * r2, 4)].reshape(512, 1024)
+            got = dot(w, cxt[...]).astype(BF)
+            for i in range(4):
+                slot = ((z + OFFSETS[4 * r2 + i] + 8) % 8) * 4 + 2 * gx + gc_
+                qkvt[pl.ds(pl.multiple_of(96 * slot, 32), 96), :] = got[128 * i : 128 * i + 96]
+                pt[pl.ds(pl.multiple_of(32 * slot, 32), 32), :] = wall[
+                    gx, gc_, 4 * r2 + i, 1, pl.ds(32, 32), :
+                ]
+
+    for k in range(5):
+        ec[k].wait_recv()
+
+    @pl.loop(0, 2)
+    def _(g):
+        project(xh, g)
+
     pass_twin(3)
     pass_twin(4)
     for k in range(5):
-        ec[k].wait_recv()
-    for k in range(5):
         gc[k].wait_recv()
 
+    @pl.loop(0, 2)
+    def _(g):
+        project(1 - xh, g)
+
+    c_lift = jnp.where(edge, F32(-1e30), F32(0.0))
+
     @pl.loop(0, 4)
-    def _(g):
-        for r2 in range(2):
-            w = wall[g // 2, g % 2, pl.ds(4 * r2, 4)].reshape(512, 1024)
-            got = dot(w, cxt[...]).astype(BF)
-            for i in range(4):
-                slot = ((z + OFFSETS[4 * r2 + i] + 8) % 8) * 4 + g
-                at = pl.multiple_of(96 * slot, 32)
-                qkvt[pl.ds(at, 96), :] = got[128 * i : 128 * i + 96]
-                pt[pl.ds(pl.multiple_of(32 * slot, 32), 32), :] = wall[
-                    g // 2, g % 2, 4 * r2 + i, 1, pl.ds(32, 32), :
-                ]
-
-    c_lift = jnp.where(edge, F32(-1e30), F32(0.0))
-
-    @pl.loop(0, 8)
     def _(j):
         bias = jnp.where(off_half, c_lift, F32(0.0))
-        at = pl.multiple_of(128 * j, 128)
-        qt = (qkvt[pl.ds(at, 128), :].astype(F32) * 0.125).astype(BF)
-        keys = qkvt[pl.ds(at + 1024, 128), :].astype(F32).T.astype(BF)
-        vt = qkvt[pl.ds(at + 2048, 128), :]
-        o = attend_pair(keys, qt, vt, bias).T
-        cm[:, :, :, pl.ds(at, 128)] = o.reshape(16, 2, 8, 128).astype(BF)
+        for i in range(2):
+            at = pl.multiple_of(256 * j + 128 * i, 128)
+            qt = (qkvt[pl.ds(at, 128), :].astype(F32) * 0.125).astype(BF)
+            keys = qkvt[pl.ds(at + 1024, 128), :].astype(F32).T.astype(BF)
+            vt = qkvt[pl.ds(at + 2048, 128), :]
+            o = attend_pair(keys, qt, vt, bias).T
+            cm[:, :, :, pl.ds(at, 128)] = o.reshape(4, 8, 8, 128).astype(BF)
 
     d = [
-        remote(cm.at[pl.ds(0, 8), 1], cmo.at[pl.ds(8, 8), 0], ds_, dr, 0, east),
-        remote(cm.at[pl.ds(8, 8), 0], cmo.at[pl.ds(0, 8), 1], ds_, dr, 1, south),
-        remote(cm.at[pl.ds(8, 8), 1], cmo.at[pl.ds(0, 8), 0], ds_, dr, 2, southeast),
+        remote(cm.at[1], cmo.at[2], ds_, dr, 0, east),
+        remote(cm.at[2], cmo.at[1], ds_, dr, 1, south),
+        remote(cm.at[3], cmo.at[0], ds_, dr, 2, southeast),
     ]
-    cmo[pl.ds(8, 8), 1] = cm[pl.ds(0, 8), 0]
+    cmo[3] = cm[0]
     for copy in d:
         copy.wait_recv()
-    mixed = cmo[...].astype(F32).reshape(256, 1024).astype(BF)
-    ot[...] = mixed
+    ot[...] = cmo[...].astype(F32).reshape(256, 1024).astype(BF)
 
     @pl.loop(0, 4)
     def _(s):
@@ -305,8 +317,9 @@
             ot[...], pt[pl.ds(at, 256), :], (((1,), (1,)), ((), ())), preferred_element_type=F32
         )
         cut = pl.ds(at, 256)
-        res = mg[:, :, :, cut].astype(F32) + got.reshape(16, 2, 8, 256)
-        co[:, :, :, cut] = res.astype(BF)
+        res = (mg[:, :, :, cut].astype(F32) + got.reshape(4, 8, 8, 256)).astype(BF)
+        for q in range(4):
+            co[pl.ds(8 * (q // 2), 8), q % 2, :, cut] = res[q]
 
     out_c = pltpu.make_async_copy(co, coarse_out, osem.at[1])
     out_c.start()
@@ -317,7 +330,6 @@
 
 
 def body(field, qkv_fine, proj_fine, up_fine, down_fine, merge_weight, qkv_coarse, proj_coarse):
-    shard = jnp.concatenate([qkv_coarse.T, proj_coarse.T], axis=0).reshape(2, 64, 1024)
     any_spec = pl.BlockSpec(memory_space=pl.ANY)
     dma = pltpu.SemaphoreType.DMA
     vm = pltpu.VMEM
@@ -327,20 +339,20 @@
             jax.ShapeDtypeStruct((32, 4, 8, 512), BF),
             jax.ShapeDtypeStruct((16, 2, 8, 1024), BF),
         ),
-        in_specs=[any_spec] * 7,
+        in_specs=[any_spec] * 8,
         out_specs=(any_spec, any_spec),
         scratch_shapes=[
             vm((512, 1536), BF), vm((512, 512), BF), vm((512, 2048), BF), vm((2048, 512), BF),
-            vm((2048, 1024), BF),
+            vm((2048, 1024), BF), vm((1024, 96), BF), vm((1024, 32), BF),
             vm((32, 4, 8, 512), BF), vm((32, 4, 8, 512), BF), vm((32, 4, 8, 512), BF),
             vm((32, 4, 8, 512), BF), vm((32, 4, 8, 512), BF),
             vm((4, 256, 128), F32), vm((256, 2048), BF),
-            vm((16, 2, 8, 1024), BF), vm((16, 2, 8, 1024), BF), vm((1024, 256), BF),
+            vm((4, 8, 8, 1024), BF), vm((4, 8, 8, 1024), BF), vm((1024, 256), BF),
             vm((2, 2, 8, 2, 64, 1024), BF), vm((3072, 256), BF), vm((256, 1024), BF),
-            vm((16, 2, 8, 1024), BF), vm((16, 2, 8, 1024), BF), vm((16, 2, 8, 1024), BF),
+            vm((4, 8, 8, 1024), BF), vm((4, 8, 8, 1024), BF), vm((16, 2, 8, 1024), BF),
             vm((1024, 1024), BF),
-            dma((8,)), dma((2,)),
-            dma((3,)), dma((3,)), dma((3,)), dma((3,)), dma((3,)), dma((3,)), dma((3,)), dma((3,)),
+            dma((9,)), dma((2,)),
+            dma((3,)), dma((3,)), dma((5,)), dma((5,)), dma((3,)), dma((3,)), dma((3,)), dma((3,)),
             dma((8,)), dma((8,)), dma((5,)), dma((5,)), dma((5,)), dma((5,)),
             dma((5,)), dma((5,)), dma((5,)), dma((5,)),
         ],
@@ -348,7 +360,8 @@
             collective_id=0, has_side_effects=True, vmem_limit_bytes=60 * 1024 * 1024
         ),
         name="encoder",
-    )(field.reshape(32, 4, 8, 512), qkv_fine, proj_fine, up_fine, down_fine, merge_weight, shard)
+    )(field.reshape(32, 4, 8, 512), qkv_fine, proj_fine, up_fine, down_fine, merge_weight,
+      qkv_coarse, proj_coarse)
     return fine.reshape(32, 32, 512), coarse.reshape(16, 16, 1024)
 
 

time: 100 us -> 85.5 us (0.85)
  Pallas kernels: 94.4 us -> 78.1 us
  local copies, waits for them, and re-layouts: 3.16 us -> 6.61 us
  other arithmetic: 1.69 us -> 0 us
    pallas_call x1, Pallas kernels: 94.4 us -> 78.1 us  [body(): pl.pallas_call(kernel, out_shape=(jax.ShapeDtypeStruct((32, 4, 8, 512), B...]
    unnamed x4 -> x6, local copies, waits for them, and re-layouts: 3.16 us -> 6.61 us
    concatenate x1 -> x0, other arithmetic: 1.69 us -> none  [body(): jnp.concatenate([qkv_coarse.T, proj_coarse.T], axis=0).reshape(2, 64, 1024)]
where the time goes in v1:
time: 85.5 us; the launch traced here: 85.4 us
  Pallas kernels  78.1 us (91%)
  local copies, waits for them, and re-layouts  6.61 us (8%)
    pallas_call x1, Pallas kernels, body(): pl.pallas_call(kernel, out_shape=(jax.ShapeDtypeStruct((32, 4, 8, 512), B...  78.1 us
    unnamed x6, local copies, waits for them, and re-layouts  6.61 us

profile of v1, /device:TPU:8, one launch (start us, length us, event | category | flops | bytes accessed | tf_op | source)
XLA Modules:
  0.0 85.4 jit_solution(14606433564123889319)
XLA Ops:
  0.6 1.8 %copy.10.cqkv_h = bf16[1024,96]{1,0:T(8,128)(2,1)} copy(bf16[1024,96]{0,1:T(8,128)(2,1)} %param.14) | data formatting | bytes 393216 | tf_op args[6]
  2.4 1.7 %copy.11.cproj_h = bf16[1024,32]{1,0:T(8,128)(2,1)} copy(bf16[1024,32]{0,1:T(8,128)(2,1)} %param.15) | data formatting | bytes 131072 | tf_op args[7]
  4.1 78.1 %encoder.1 = (bf16[32,4,8,512]{3,2,1,0:T(8,128)(2,1)}, bf16[16,2,8,1024]{3,2,1,0:T(8,128)(2,1)}) custom-call(bf16[32,4,8,512]{3,2,1,0:T(8,128)(2,1)} %bitcast.3, bf16[512,1536]{1,0:T(8,128)(2,1)} %wqkv_h.1, bf16[512,512]{1,0:T(8,128)(2,1)} %wproj_h.1, bf16[512,2048]{1,0:T(8,128)(2,1)} %wup_h.1, bf16[2048,512]{1,0:T(8,128)(2,1)} %wdown_h.1, ...), custom_call_target="tpu_custom_call" | custom-call | tf_op jit(solution)/shard_map/encoder/pallas_call | solution.py:336
  82.2 0.0 copy-start
  82.2 2.4 %copy.14 = bf16[32,32,512]{2,1,0:T(8,128)(2,1)} copy(bf16[32,32,512]{2,1,0:T(8,128)(2,1)} %bitcast.4) | data formatting | bytes 2097152
  84.6 0.0 copy-done
  84.6 0.8 copy.15
Async XLA Ops:
  82.2 2.4 %copy-start = (bf16[16,2,8,1024]{3,2,1,0:T(8,128)(2,1)S(1)}, bf16[16,2,8,1024]{3,2,1,0:T(8,128)(2,1)}, u32[]{:S(2)}) copy-start(bf16[16,2,8,1024]{3,2,1,0:T(8,128)(2,1)} %get-tuple-element.5) | copy-start | bytes 1572868

commit v2 on v1

--- a/solution.py
+++ b/solution.py
@@ -9,7 +9,8 @@
 BF = jnp.bfloat16
 F32 = jnp.float32
 OFFSETS = (0, -1, 1, -2, 2, -3, 3, 4)
-CHUNKS = ((0, 1), (1, 2), (3, 2), (5, 2), (7, 1))
+CHUNKS = ((0, 1), (1, 2), (3, 2), (5, 1), (6, 1), (7, 1))
+LAST = len(CHUNKS)
 
 
 def norm(v):
@@ -39,10 +40,11 @@
 
 def kernel(
     field, wqkv_h, wproj_h, wup_h, wdown_h, wmerge_h, cqkv_h, cproj_h,
-    fine_out, coarse_out,
-    wqkv, wproj, wup, wdown, wmerge, cqkv, cproj,
-    fv, xr, mr, mo, fo, fs, jn, mg, cr, cxt, wall, qkvt, ot, cm, cmo, co, pt,
-    lsem, osem, hs, hr, bs, br, cs, cq, ds_, dr, zs, zr, xs, xq, ps, pr, es, er, gs, gr,
+    fo, mg, ot, pt,
+    wqkv, wproj, wup, wdown, wmerge,
+    fv, xr, mr, mo, fs, jn, cr, cxt, wall, pall, qkvt, cm, cmo,
+    lsem, hs, hr, bs, br, cs, cq, ds_, dr, zs, zr, xs, xq, ps, pr, es, er, gs, gr,
+    zs2, zr2, xs2, xq2, ps2, pr2, es2, er2, gs2, gr2,
 ):
     lat = lax.axis_index("lat")
     lon = lax.axis_index("lon")
@@ -80,8 +82,8 @@
         return copy
 
     own_x = local(field.at[pl.ds(8, 24), pl.ds(1, 3)], xr.at[pl.ds(0, 24), pl.ds(0, 3)], 0)
-    own_q = local(cqkv_h, cqkv, 7)
-    own_p = local(cproj_h, cproj, 8)
+    own_q = local(cqkv_h, wall.at[xh, c, 0], 7)
+    own_p = local(cproj_h, pall.at[xh, c, 0], 8)
     l_qkv = local(wqkv_h, wqkv, 1)
     own_f = local(field, fv, 2)
     l_proj = local(wproj_h, wproj, 3)
@@ -101,57 +103,74 @@
         remote(field.at[pl.ds(0, 8), 0], xr.at[pl.ds(24, 8), 3], hs, hr, 2, northwest),
     ]
 
-    zc, xc, pc, ec, gc = {}, {}, {}, {}, {}
-
-    def send_z(step):
-        if step == 0:
-            zc[0] = remote(wall.at[xh, c, 0], wall.at[xh, c, 1], zs, zr, 0, zup)
-            zc[1] = remote(wall.at[xh, c, 0], wall.at[xh, c, 2], zs, zr, 1, zdn)
-        elif step < 3:
-            a = 2 * step
-            zc[a] = remote(wall.at[xh, c, a - 1], wall.at[xh, c, a + 1], zs, zr, a, zup)
-            zc[a + 1] = remote(wall.at[xh, c, a], wall.at[xh, c, a + 2], zs, zr, a + 1, zdn)
-        else:
-            zc[6] = remote(wall.at[xh, c, 5, 0], wall.at[xh, c, 7, 0], zs, zr, 6, zup)
-            zc[7] = remote(wall.at[xh, c, 6, 1], wall.at[xh, c, 7, 1], zs, zr, 7, zdn)
-
-    def own_chunk(k):
-        at, n = CHUNKS[k]
-        half = wall.at[xh, c, pl.ds(at, n), xlo]
-        full = wall.at[xh, c, pl.ds(at, n)]
-        xc[k] = remote(half, half, xs, xq, k, cross)
-        ec[k] = remote(full, full, es, er, k, twin)
-
-    def pass_cross(k):
-        at, n = CHUNKS[k]
-        xc[k].wait_recv()
-        ref = wall.at[1 - xh, c, pl.ds(at, n), 1 - xlo]
-        pc[k] = remote(ref, ref, ps, pr, k, pair)
-
-    def pass_twin(k):
-        at, n = CHUNKS[k]
-        pc[k].wait_recv()
-        ref = wall.at[1 - xh, c, pl.ds(at, n)]
-        gc[k] = remote(ref, ref, gs, gr, k, twin)
+    class Gather:
+        def __init__(self, wall, zs, zr, xs, xq, ps, pr, es, er, gs, gr):
+            self.wall = wall
+            self.sems = dict(z=(zs, zr), x=(xs, xq), p=(ps, pr), e=(es, er), g=(gs, gr))
+            self.made = dict(z={}, x={}, p={}, e={}, g={})
+
+        def send(self, kind, at, src, dst, device):
+            self.made[kind][at] = remote(src, dst, *self.sems[kind], at, device)
+
+        def arrive(self, kind, *ats):
+            for at in ats:
+                self.made[kind][at].wait_recv()
+
+        def send_z(self, step):
+            own = self.wall.at[xh, c]
+            if step == 0:
+                self.send("z", 0, own.at[0], own.at[1], zup)
+                self.send("z", 1, own.at[0], own.at[2], zdn)
+            elif step < 3:
+                a = 2 * step
+                self.send("z", a, own.at[a - 1], own.at[a + 1], zup)
+                self.send("z", a + 1, own.at[a], own.at[a + 2], zdn)
+            else:
+                self.send("z", 6, own.at[5, 0], own.at[7, 0], zup)
+                self.send("z", 7, own.at[6, 1], own.at[7, 1], zdn)
+
+        def own_chunk(self, k):
+            at, n = CHUNKS[k]
+            half = self.wall.at[xh, c, pl.ds(at, n), xlo]
+            full = self.wall.at[xh, c, pl.ds(at, n)]
+            self.send("x", k, half, half, cross)
+            self.send("e", k, full, full, twin)
+
+        def pass_cross(self, *ks):
+            for k in ks:
+                at, n = CHUNKS[k]
+                self.arrive("x", k)
+                ref = self.wall.at[1 - xh, c, pl.ds(at, n), 1 - xlo]
+                self.send("p", k, ref, ref, pair)
+
+        def pass_twin(self, *ks):
+            for k in ks:
+                at, n = CHUNKS[k]
+                self.arrive("p", k)
+                ref = self.wall.at[1 - xh, c, pl.ds(at, n)]
+                self.send("g", k, ref, ref, twin)
+
+        def start(self):
+            self.send_z(0)
+            self.own_chunk(0)
+
+        def forward(self, k):
+            self.arrive("z", 2 * k - 2, 2 * k - 1)
+            if k < 4:
+                self.send_z(k)
+            for chunk in ((1,), (2,), (3, 4), (5,))[k - 1]:
+                self.own_chunk(chunk)
+            if k < 4:
+                self.pass_cross(k - 1)
+            if k >= 2:
+                self.pass_twin(k - 2)
+
+    main = Gather(wall, zs, zr, xs, xq, ps, pr, es, er, gs, gr)
+    tail = Gather(pall, zs2, zr2, xs2, xq2, ps2, pr2, es2, er2, gs2, gr2)
 
     own_q.wait()
     own_p.wait()
-    for t in range(4):
-        rows = slice(256 * t, 256 * t + 256)
-        shard = jnp.concatenate([cqkv[rows, :].astype(F32), cproj[rows, :].astype(F32)], axis=1)
-        wall[xh, c, 0, :, :, rows] = shard.T.astype(BF).reshape(2, 64, 256)
-    send_z(0)
-    own_chunk(0)
-
-    def forward(k):
-        zc[2 * k - 2].wait_recv()
-        zc[2 * k - 1].wait_recv()
-        if k < 4:
-            send_z(k)
-        own_chunk(k)
-        pass_cross(k - 1)
-        if k >= 2:
-            pass_twin(k - 2)
+    main.start()
 
     off_half = (lax.broadcasted_iota(jnp.int32, (256, 256), 0) >= 128) != (
         lax.broadcasted_iota(jnp.int32, (256, 256), 1) >= 128
@@ -183,14 +202,15 @@
     b = [remote(mr.at[pl.ds(0, 16), 3], mo.at[pl.ds(8, 16), 0], bs, br, 0, east)]
     h[1].wait_recv()
     h[2].wait_recv()
-    forward(1)
+    main.forward(1)
     fine_window(1, 0)
     b.append(remote(mr.at[pl.ds(24, 8), pl.ds(0, 2)], mo.at[pl.ds(0, 8), pl.ds(1, 2)], bs, br, 1, south))
     fine_window(1, 1)
     b.append(remote(mr.at[pl.ds(16, 8), 3], mo.at[pl.ds(24, 8), 0], bs, br, 2, east))
     b.append(remote(mr.at[pl.ds(24, 8), 2], mo.at[pl.ds(0, 8), 3], bs, br, 3, south))
     b.append(remote(mr.at[pl.ds(24, 8), 3], mo.at[pl.ds(0, 8), 0], bs, br, 4, southeast))
-    forward(2)
+    main.forward(2)
+    tail.start()
     mo[pl.ds(8, 24), pl.ds(1, 3)] = mr[pl.ds(0, 24), pl.ds(0, 3)]
     for copy in (own_f, l_proj, l_up, l_down, l_merge):
         copy.wait()
@@ -242,7 +262,8 @@
     for at in (1, 3, 4):
         b[at].wait_recv()
     fine_quarter(0, 1)
-    forward(3)
+    main.forward(3)
+    tail.forward(1)
     fine_quarter(0, 0)
     merge(0, 3)
     a = [
@@ -250,65 +271,84 @@
         remote(mg.at[1], cr.at[2], cs, cq, 1, north),
         remote(mg.at[0], cr.at[3], cs, cq, 2, northwest),
     ]
-    out_f = pltpu.make_async_copy(fo, fine_out, osem.at[0])
-    out_f.start()
-    forward(4)
+    main.forward(4)
+    main.pass_cross(3)
+    tail.forward(2)
     merge(3, 1)
     cr[0] = mg[3]
-    pass_cross(4)
+    main.pass_cross(4, 5)
     for copy in a:
         copy.wait_recv()
+    main.pass_twin(3)
+    tail.forward(3)
     cxt[...] = norm(cr[...].astype(F32).reshape(256, 1024)).T.astype(BF)
 
     def project(gx, gc_):
         for r2 in range(2):
-            w = wall[gx, gc_, pl.ds(4 * r2, 4)].reshape(512, 1024)
+            w = wall[gx, gc_, pl.ds(4 * r2, 4)].reshape(384, 1024)
             got = dot(w, cxt[...]).astype(BF)
             for i in range(4):
                 slot = ((z + OFFSETS[4 * r2 + i] + 8) % 8) * 4 + 2 * gx + gc_
-                qkvt[pl.ds(pl.multiple_of(96 * slot, 32), 96), :] = got[128 * i : 128 * i + 96]
-                pt[pl.ds(pl.multiple_of(32 * slot, 32), 32), :] = wall[
-                    gx, gc_, 4 * r2 + i, 1, pl.ds(32, 32), :
-                ]
-
-    for k in range(5):
-        ec[k].wait_recv()
+                qkvt[pl.ds(pl.multiple_of(96 * slot, 32), 96), :] = got[96 * i : 96 * i + 96]
+
+    main.arrive("e", *range(LAST))
 
     @pl.loop(0, 2)
     def _(g):
         project(xh, g)
 
-    pass_twin(3)
-    pass_twin(4)
-    for k in range(5):
-        gc[k].wait_recv()
-
-    @pl.loop(0, 2)
+    main.pass_twin(4, 5)
+    tail.forward(4)
+    project(1 - xh, c)
+    main.arrive("g", *range(LAST))
+    project(1 - xh, 1 - c)
+    tail.pass_cross(3, 4, 5)
+
+    c_lift = jnp.where(edge, F32(-1e30), F32(0.0))
+
+    def coarse_heads(first):
+        @pl.loop(first, first + 2)
+        def _(j):
+            bias = jnp.where(off_half, c_lift, F32(0.0))
+            for i in range(2):
+                at = pl.multiple_of(256 * j + 128 * i, 128)
+                qt = (qkvt[pl.ds(at, 128), :].astype(F32) * 0.125).astype(BF)
+                keys = qkvt[pl.ds(at + 1024, 128), :].astype(F32).T.astype(BF)
+                vt = qkvt[pl.ds(at + 2048, 128), :]
+                o = attend_pair(keys, qt, vt, bias).T
+                cm[:, :, :, pl.ds(at, 128)] = o.reshape(4, 8, 8, 128).astype(BF)
+
+    d = []
+    for part in range(2):
+        coarse_heads(2 * part)
+        if part == 0:
+            tail.pass_twin(3, 4, 5)
+        cut = pl.ds(512 * part, 512)
+        for i, (src, dst, device) in enumerate(((1, 2, east), (2, 1, south), (3, 0, southeast))):
+            d.append(
+                remote(cm.at[src, :, :, cut], cmo.at[dst, :, :, cut], ds_, dr, 3 * part + i, device)
+            )
+    cmo[3] = cm[0]
+    tail.arrive("e", *range(LAST))
+    tail.arrive("g", *range(LAST))
+
+    @pl.loop(0, 4)
     def _(g):
-        project(1 - xh, g)
-
-    c_lift = jnp.where(edge, F32(-1e30), F32(0.0))
-
-    @pl.loop(0, 4)
-    def _(j):
-        bias = jnp.where(off_half, c_lift, F32(0.0))
-        for i in range(2):
-            at = pl.multiple_of(256 * j + 128 * i, 128)
-            qt = (qkvt[pl.ds(at, 128), :].astype(F32) * 0.125).astype(BF)
-            keys = qkvt[pl.ds(at + 1024, 128), :].astype(F32).T.astype(BF)
-            vt = qkvt[pl.ds(at + 2048, 128), :]
-            o = attend_pair(keys, qt, vt, bias).T
-            cm[:, :, :, pl.ds(at, 128)] = o.reshape(4, 8, 8, 128).astype(BF)
-
-    d = [
-        remote(cm.at[1], cmo.at[2], ds_, dr, 0, east),
-        remote(cm.at[2], cmo.at[1], ds_, dr, 1, south),
-        remote(cm.at[3], cmo.at[0], ds_, dr, 2, southeast),
-    ]
-    cmo[3] = cm[0]
+        for r in range(8):
+            slot = ((z + OFFSETS[r] + 8) % 8) * 4 + g
+            pt[pl.ds(pl.multiple_of(32 * slot, 32), 32), :] = pall[g // 2, g % 2, r].reshape(32, 1024)
+
     for copy in d:
         copy.wait_recv()
     ot[...] = cmo[...].astype(F32).reshape(256, 1024).astype(BF)
+
+    for copy in sent:
+        copy.wait_send()
+
+
+def finish(fo, mg, ot, pt, fine_out, coarse_out, co, osem):
+    out_f = pltpu.make_async_copy(fo, fine_out, osem.at[0])
+    out_f.start()
 
     @pl.loop(0, 4)
     def _(s):
@@ -323,45 +363,57 @@
 
     out_c = pltpu.make_async_copy(co, coarse_out, osem.at[1])
     out_c.start()
-    for copy in sent:
-        copy.wait_send()
     out_f.wait()
     out_c.wait()
 
 
 def body(field, qkv_fine, proj_fine, up_fine, down_fine, merge_weight, qkv_coarse, proj_coarse):
-    any_spec = pl.BlockSpec(memory_space=pl.ANY)
+    any_spec = pl.BlockSpec(memory_space=pltpu.HBM)
     dma = pltpu.SemaphoreType.DMA
     vm = pltpu.VMEM
+    in_vmem = pl.BlockSpec(memory_space=pltpu.VMEM)
+    held = pl.pallas_call(
+        kernel,
+        out_shape=(
+            pltpu.VMEM((32, 4, 8, 512), BF),
+            pltpu.VMEM((4, 8, 8, 1024), BF),
+            pltpu.VMEM((256, 1024), BF),
+            pltpu.VMEM((1024, 1024), BF),
+        ),
+        in_specs=[any_spec] * 8,
+        out_specs=(in_vmem,) * 4,
+        scratch_shapes=[
+            vm((512, 1536), BF), vm((512, 512), BF), vm((512, 2048), BF), vm((2048, 512), BF),
+            vm((2048, 1024), BF),
+            vm((32, 4, 8, 512), BF), vm((32, 4, 8, 512), BF), vm((32, 4, 8, 512), BF),
+            vm((32, 4, 8, 512), BF),
+            vm((4, 256, 128), F32), vm((256, 2048), BF),
+            vm((4, 8, 8, 1024), BF), vm((1024, 256), BF),
+            vm((2, 2, 8, 2, 48, 1024), BF), vm((2, 2, 8, 2, 16, 1024), BF), vm((3072, 256), BF),
+            vm((4, 8, 8, 1024), BF), vm((4, 8, 8, 1024), BF),
+            dma((9,)),
+            *[dma((n,)) for n in (3, 3, 5, 5, 3, 3, 6, 6)],
+            *[dma((n,)) for n in (8, 8, 6, 6, 6, 6, 6, 6, 6, 6)],
+            *[dma((n,)) for n in (8, 8, 6, 6, 6, 6, 6, 6, 6, 6)],
+        ],
+        compiler_params=pltpu.CompilerParams(
+            collective_id=0, has_side_effects=True, vmem_limit_bytes=59 * 1024 * 1024
+        ),
+        name="encoder",
+    )(field.reshape(32, 4, 8, 512), qkv_fine, proj_fine, up_fine, down_fine, merge_weight,
+      qkv_coarse.T.reshape(2, 48, 1024), proj_coarse.T.reshape(2, 16, 1024))
     fine, coarse = pl.pallas_call(
-        kernel,
+        finish,
         out_shape=(
             jax.ShapeDtypeStruct((32, 4, 8, 512), BF),
             jax.ShapeDtypeStruct((16, 2, 8, 1024), BF),
         ),
-        in_specs=[any_spec] * 8,
+        in_specs=[in_vmem] * 4,
         out_specs=(any_spec, any_spec),
-        scratch_shapes=[
-            vm((512, 1536), BF), vm((512, 512), BF), vm((512, 2048), BF), vm((2048, 512), BF),
-            vm((2048, 1024), BF), vm((1024, 96), BF), vm((1024, 32), BF),
-            vm((32, 4, 8, 512), BF), vm((32, 4, 8, 512), BF), vm((32, 4, 8, 512), BF),
-            vm((32, 4, 8, 512), BF), vm((32, 4, 8, 512), BF),
-            vm((4, 256, 128), F32), vm((256, 2048), BF),
-            vm((4, 8, 8, 1024), BF), vm((4, 8, 8, 1024), BF), vm((1024, 256), BF),
-            vm((2, 2, 8, 2, 64, 1024), BF), vm((3072, 256), BF), vm((256, 1024), BF),
-            vm((4, 8, 8, 1024), BF), vm((4, 8, 8, 1024), BF), vm((16, 2, 8, 1024), BF),
-            vm((1024, 1024), BF),
-            dma((9,)), dma((2,)),
-            dma((3,)), dma((3,)), dma((5,)), dma((5,)), dma((3,)), dma((3,)), dma((3,)), dma((3,)),
-            dma((8,)), dma((8,)), dma((5,)), dma((5,)), dma((5,)), dma((5,)),
-            dma((5,)), dma((5,)), dma((5,)), dma((5,)),
-        ],
-        compiler_params=pltpu.CompilerParams(
-            collective_id=0, has_side_effects=True, vmem_limit_bytes=60 * 1024 * 1024
-        ),
-        name="encoder",
-    )(field.reshape(32, 4, 8, 512), qkv_fine, proj_fine, up_fine, down_fine, merge_weight,
-      qkv_coarse, proj_coarse)
+        scratch_shapes=[vm((16, 2, 8, 1024), BF), dma((2,))],
+        compiler_params=pltpu.CompilerParams(vmem_limit_bytes=8 * 1024 * 1024),
+        name="finish",
+    )(*held)
     return fine.reshape(32, 32, 512), coarse.reshape(16, 16, 1024)
 
 

time: 85.5 us -> 74.7 us (0.87)
  local copies, waits for them, and re-layouts: 6.61 us -> 0 us
  Pallas kernels: 78.1 us -> 73.6 us
    unnamed x6 -> x0, local copies, waits for them, and re-layouts: 6.61 us -> none
    pallas_call x1 -> x2, Pallas kernels: 78.1 us -> 73.6 us  [the longest x1 71.4 us: body(): pl.pallas_call(kernel, out_shape=(pltpu.VMEM((32, 4, 8, 512), BF), pltpu....]
where the time goes in v2:
time: 74.7 us; the launch traced here: 74.4 us
  Pallas kernels  73.6 us (99%)
  between operations  0.8 us (1%)
    pallas_call x1, Pallas kernels, body(): pl.pallas_call(kernel, out_shape=(pltpu.VMEM((32, 4, 8, 512), BF), pltpu....  71.4 us
    pallas_call x1, Pallas kernels, body(): pl.pallas_call(finish, out_shape=(jax.ShapeDtypeStruct((32, 4, 8, 512), B...  2.17 us

profile of v2, /device:TPU:8, one launch (start us, length us, event | category | flops | bytes accessed | tf_op | source)
XLA Modules:
  0.0 74.4 jit_solution(14381976169445573032)
XLA Ops:
  0.6 71.4 %encoder.1 = (bf16[32,4,8,512]{3,2,1,0:T(8,128)(2,1)S(1)}, bf16[4,8,8,1024]{3,2,1,0:T(8,128)(2,1)S(1)}, bf16[256,1024]{1,0:T(8,128)(2,1)S(1)}, bf16[1024,1024]{1,0:T(8,128)(2,1)S(1)}) custom-call(bf16[32,4,8,512]{3,2,1,0:T(8,128)(2,1)} %bitcast.9, bf16[512,1536]{1,0:T(8,128)(2,1)} %wqkv_h.1, bf16[512,512]{1,0:T(8,128)(2,1)} %wproj_h.1, ...), custom_call_target="tpu_custom_call" | custom-call | tf_op jit(solution)/shard_map/encoder/pallas_call | solution.py:375
  72.1 2.2 %finish.1 = (bf16[32,4,8,512]{3,2,1,0:T(8,128)(2,1)}, bf16[16,2,8,1024]{3,2,1,0:T(8,128)(2,1)}) custom-call(bf16[32,4,8,512]{3,2,1,0:T(8,128)(2,1)S(1)} %get-tuple-element.8.fo, bf16[4,8,8,1024]{3,2,1,0:T(8,128)(2,1)S(1)} %get-tuple-element.9.mg, bf16[256,1024]{1,0:T(8,128)(2,1)S(1)} %get-tuple-element.10.ot, bf16[1024,1024]{1,0:T(8,128)(2,1)S(1)} %get-tuple-element.11.pt), custom_call_target="tpu_custom_call" | custom-call | tf_op jit(solution)/shard_map/finish/pallas_call | solution.py:405

commit v3 on v2

--- a/solution.py
+++ b/solution.py
@@ -8,6 +8,7 @@
 MESH = pl.DeviceIdType.MESH
 BF = jnp.bfloat16
 F32 = jnp.float32
+SCALE = 0.125 * 1.4426950408889634
 OFFSETS = (0, -1, 1, -2, 2, -3, 3, 4)
 CHUNKS = ((0, 1), (1, 2), (3, 2), (5, 1), (6, 1), (7, 1))
 LAST = len(CHUNKS)
@@ -29,9 +30,11 @@
     for half in range(2):
         part = qt[64 * half : 64 * half + 64]
         padded = jnp.concatenate([part, zero] if half == 0 else [zero, part], axis=0)
-        scores = dot(keys, padded) + bias
+        scores = dot(keys, padded)
+        if bias is not None:
+            scores = scores + bias
         top = jnp.max(scores, axis=0, keepdims=True)
-        p = jnp.exp(scores - top)
+        p = jnp.exp2(scores - top)
         total = jnp.sum(p, axis=0, keepdims=True)
         o = dot(vt[64 * half : 64 * half + 64], p.astype(BF))
         outs.append(o * (1.0 / total))
@@ -162,7 +165,7 @@
                 self.own_chunk(chunk)
             if k < 4:
                 self.pass_cross(k - 1)
-            if k >= 2:
+            if 2 <= k < 4:
                 self.pass_twin(k - 2)
 
     main = Gather(wall, zs, zr, xs, xq, ps, pr, es, er, gs, gr)
@@ -175,14 +178,13 @@
     off_half = (lax.broadcasted_iota(jnp.int32, (256, 256), 0) >= 128) != (
         lax.broadcasted_iota(jnp.int32, (256, 256), 1) >= 128
     )
-    edge = lat == 7
+    lift = jnp.where(lat == 7, F32(-1e30), F32(0.0))
 
     def fine_window(wr, wc):
-        lift = jnp.where(jnp.logical_and(edge, wr == 1), F32(-1e30), F32(0.0))
-        bias = jnp.where(off_half, lift, F32(0.0))
+        bias = jnp.where(off_half, lift, F32(0.0)) if wr == 1 else None
         x = xr[pl.ds(16 * wr, 16), pl.ds(2 * wc, 2)].astype(F32).reshape(256, 512)
         xn = norm(x).astype(BF)
-        q = (dot(xn, wqkv[:, 0:512])).astype(BF).astype(F32) * 0.125
+        q = dot(xn, wqkv[:, 0:512]) * SCALE
         keys = dot(xn, wqkv[:, 512:1024]).astype(BF)
         v = dot(xn, wqkv[:, 1024:1536])
         qt = q.T.astype(BF)
@@ -210,7 +212,6 @@
     b.append(remote(mr.at[pl.ds(24, 8), 2], mo.at[pl.ds(0, 8), 3], bs, br, 3, south))
     b.append(remote(mr.at[pl.ds(24, 8), 3], mo.at[pl.ds(0, 8), 0], bs, br, 4, southeast))
     main.forward(2)
-    tail.start()
     mo[pl.ds(8, 24), pl.ds(1, 3)] = mr[pl.ds(0, 24), pl.ds(0, 3)]
     for copy in (own_f, l_proj, l_up, l_down, l_merge):
         copy.wait()
@@ -259,19 +260,21 @@
     b[0].wait_recv()
     b[2].wait_recv()
     fine_quarter(1, 0)
+    main.forward(3)
+    tail.start()
     for at in (1, 3, 4):
         b[at].wait_recv()
     fine_quarter(0, 1)
-    main.forward(3)
+    fine_quarter(0, 0)
+    main.forward(4)
     tail.forward(1)
-    fine_quarter(0, 0)
     merge(0, 3)
     a = [
         remote(mg.at[2], cr.at[1], cs, cq, 0, west),
         remote(mg.at[1], cr.at[2], cs, cq, 1, north),
         remote(mg.at[0], cr.at[3], cs, cq, 2, northwest),
     ]
-    main.forward(4)
+    main.pass_twin(2)
     main.pass_cross(3)
     tail.forward(2)
     merge(3, 1)
@@ -280,8 +283,8 @@
     for copy in a:
         copy.wait_recv()
     main.pass_twin(3)
+    cxt[...] = norm(cr[...].astype(F32).reshape(256, 1024)).T.astype(BF)
     tail.forward(3)
-    cxt[...] = norm(cr[...].astype(F32).reshape(256, 1024)).T.astype(BF)
 
     def project(gx, gc_):
         for r2 in range(2):
@@ -299,35 +302,30 @@
 
     main.pass_twin(4, 5)
     tail.forward(4)
+    tail.pass_twin(2)
     project(1 - xh, c)
     main.arrive("g", *range(LAST))
     project(1 - xh, 1 - c)
-    tail.pass_cross(3, 4, 5)
-
-    c_lift = jnp.where(edge, F32(-1e30), F32(0.0))
-
-    def coarse_heads(first):
-        @pl.loop(first, first + 2)
-        def _(j):
-            bias = jnp.where(off_half, c_lift, F32(0.0))
-            for i in range(2):
-                at = pl.multiple_of(256 * j + 128 * i, 128)
-                qt = (qkvt[pl.ds(at, 128), :].astype(F32) * 0.125).astype(BF)
-                keys = qkvt[pl.ds(at + 1024, 128), :].astype(F32).T.astype(BF)
-                vt = qkvt[pl.ds(at + 2048, 128), :]
-                o = attend_pair(keys, qt, vt, bias).T
-                cm[:, :, :, pl.ds(at, 128)] = o.reshape(4, 8, 8, 128).astype(BF)
-
+
+    c_bias = jnp.where(off_half, lift, F32(0.0))
     d = []
-    for part in range(2):
-        coarse_heads(2 * part)
-        if part == 0:
-            tail.pass_twin(3, 4, 5)
-        cut = pl.ds(512 * part, 512)
+    for part in range(4):
+        for i in range(2):
+            at = 256 * part + 128 * i
+            qt = (qkvt[at : at + 128, :].astype(F32) * SCALE).astype(BF)
+            keys = qkvt[at + 1024 : at + 1152, :].astype(F32).T.astype(BF)
+            vt = qkvt[at + 2048 : at + 2176, :]
+            o = attend_pair(keys, qt, vt, c_bias).T
+            cm[:, :, :, at : at + 128] = o.reshape(4, 8, 8, 128).astype(BF)
+        cut = pl.ds(256 * part, 256)
         for i, (src, dst, device) in enumerate(((1, 2, east), (2, 1, south), (3, 0, southeast))):
             d.append(
                 remote(cm.at[src, :, :, cut], cmo.at[dst, :, :, cut], ds_, dr, 3 * part + i, device)
             )
+        if part == 0:
+            tail.pass_cross(3, 4, 5)
+        if part == 3:
+            tail.pass_twin(3, 4, 5)
     cmo[3] = cm[0]
     tail.arrive("e", *range(LAST))
     tail.arrive("g", *range(LAST))
@@ -392,7 +390,7 @@
             vm((2, 2, 8, 2, 48, 1024), BF), vm((2, 2, 8, 2, 16, 1024), BF), vm((3072, 256), BF),
             vm((4, 8, 8, 1024), BF), vm((4, 8, 8, 1024), BF),
             dma((9,)),
-            *[dma((n,)) for n in (3, 3, 5, 5, 3, 3, 6, 6)],
+            *[dma((n,)) for n in (3, 3, 5, 5, 3, 3, 12, 12)],
             *[dma((n,)) for n in (8, 8, 6, 6, 6, 6, 6, 6, 6, 6)],
             *[dma((n,)) for n in (8, 8, 6, 6, 6, 6, 6, 6, 6, 6)],
         ],

time: 74.7 us -> 74.2 us (level)
  Pallas kernels: 73.6 us -> 72.8 us
    pallas_call x1, Pallas kernels: 71.4 us -> 70.6 us  [body(): pl.pallas_call(kernel, out_shape=(pltpu.VMEM((32, 4, 8, 512), BF), pltpu....]
where the time goes in v3:
time: 74.2 us; the launch traced here: 73.6 us
  Pallas kernels  72.8 us (98%)
  between operations  0.8 us (1%)
    pallas_call x1, Pallas kernels, body(): pl.pallas_call(kernel, out_shape=(pltpu.VMEM((32, 4, 8, 512), BF), pltpu....  70.6 us
    pallas_call x1, Pallas kernels, body(): pl.pallas_call(finish, out_shape=(jax.ShapeDtypeStruct((32, 4, 8, 512), B...  2.17 us

profile of v3, /device:TPU:8, one launch (start us, length us, event | category | flops | bytes accessed | tf_op | source)
XLA Modules:
  0.0 73.6 jit_solution(9919936523365812333)
XLA Ops:
  0.6 70.6 %encoder.1 = (bf16[32,4,8,512]{3,2,1,0:T(8,128)(2,1)S(1)}, bf16[4,8,8,1024]{3,2,1,0:T(8,128)(2,1)S(1)}, bf16[256,1024]{1,0:T(8,128)(2,1)S(1)}, bf16[1024,1024]{1,0:T(8,128)(2,1)S(1)}) custom-call(bf16[32,4,8,512]{3,2,1,0:T(8,128)(2,1)} %bitcast.9, bf16[512,1536]{1,0:T(8,128)(2,1)} %wqkv_h.1, bf16[512,512]{1,0:T(8,128)(2,1)} %wproj_h.1, ...), custom_call_target="tpu_custom_call" | custom-call | tf_op jit(solution)/shard_map/encoder/pallas_call | solution.py:373
  71.3 2.2 %finish.1 = (bf16[32,4,8,512]{3,2,1,0:T(8,128)(2,1)}, bf16[16,2,8,1024]{3,2,1,0:T(8,128)(2,1)}) custom-call(bf16[32,4,8,512]{3,2,1,0:T(8,128)(2,1)S(1)} %get-tuple-element.8.fo, bf16[4,8,8,1024]{3,2,1,0:T(8,128)(2,1)S(1)} %get-tuple-element.9.mg, bf16[256,1024]{1,0:T(8,128)(2,1)S(1)} %get-tuple-element.10.ot, bf16[1024,1024]{1,0:T(8,128)(2,1)S(1)} %get-tuple-element.11.pt), custom_call_target="tpu_custom_call" | custom-call | tf_op jit(solution)/shard_map/finish/pallas_call | solution.py:403
